TPU v7x, 32 devices: a whole 2x2x4 slice. The times are simulated.
32 devices in a mesh: row: 8 (over z, y), ta: 4 (over x, core).
Axes of the slice: x: 2, y: 2, z: 4, core: 2. Of those that a mesh axis runs over, the one named last changes fastest.
Arguments:
- hidden: bfloat16 [8, 256, 3584], P('row', None, 'ta'), may hold values from -6 to 6
- target: bfloat16 [8, 256, 3584], P('row', None, 'ta'), may hold values from -6 to 6
- w_down: bfloat16 [8, 2, 3584, 256], P('row', None, 'ta'), may hold values from -5 to 5
- w_up: bfloat16 [8, 2, 256, 3584], P('row', None, None, 'ta'), may hold values from -5 to 5
- m_down: float32 [8, 2, 3584, 256], P('row', None, 'ta'), may hold values from -9 to 9
- m_up: float32 [8, 2, 256, 3584], P('row', None, None, 'ta'), may hold values from -9 to 9
Outputs:
- avg_down: bfloat16 [2, 3584, 256], P(None, 'ta')
- avg_up: bfloat16 [2, 256, 3584], P(None, None, 'ta')
- mom_down: float32 [2, 3584, 256], P(None, 'ta')
- mom_up: float32 [2, 256, 3584], P(None, None, 'ta')
All inputs are finite; a program needn't handle non-finite values.
Results may differ from a plain program's by a relative error of at most 0.019.
Values may be sent and summed in bfloat16 or wider, within the bound.
A program may use at most 128 MiB of HBM per device.

v0:
```python
import jax
import jax.numpy as jnp
from jax import lax
from jax.sharding import PartitionSpec as P

D = 3584
RANK = 256
STEPS = 4


norm_eps = 1e-06
learn_rate = 0.02
moment_decay = 0.9


def contract(matrix_a, matrix_b, dim_a, dim_b):
    return lax.dot_general(
        matrix_a, matrix_b, (((dim_a,), (dim_b,)), ((), ())), preferred_element_type=jnp.float32
    )


def silu_slope(preact):
    sigmoid_v = jax.nn.sigmoid(preact)
    return sigmoid_v * (1.0 + preact * (1.0 - sigmoid_v))


def forward_layer(hidden, weights):
    w_down, w_up = weights
    wide_rows = hidden.astype(jnp.float32)
    squares = jnp.sum(wide_rows * wide_rows, axis=1)
    partial_value = jnp.dot(hidden, w_down, preferred_element_type=jnp.float32) * D ** (-0.5)
    projected, total_sq = lax.psum((partial_value, squares), "ta")
    root_mean = jnp.sqrt(total_sq / D + norm_eps)[:, None]
    preact = projected / root_mean
    activation = jax.nn.silu(preact).astype(jnp.bfloat16)
    lifted = jnp.dot(activation, w_up, preferred_element_type=jnp.float32) * RANK ** (-0.5)
    outcome = (wide_rows + lifted).astype(jnp.bfloat16)
    return (outcome, (hidden, root_mean, preact, activation))


def backward_layer(gradient, inputs):
    stored, weights, moments = inputs
    hidden, root_mean, preact, activation = stored
    w_down, w_up = weights
    grad_low = gradient.astype(jnp.bfloat16)
    grad_up = contract(activation, grad_low, 0, 0) * RANK ** (-0.5)
    grad_act = lax.psum(
        (contract(grad_low, w_up, 1, 1) * RANK ** (-0.5)).astype(jnp.bfloat16), "ta"
    ).astype(jnp.float32)
    grad_pre = grad_act * silu_slope(preact)
    row_dot = jnp.sum(grad_pre * preact, axis=1, keepdims=True)
    grad_proj = (grad_pre / root_mean).astype(jnp.bfloat16)
    grad_down = contract(hidden, grad_proj, 0, 0) * D ** (-0.5)
    wide_rows = hidden.astype(jnp.float32)
    through = contract(grad_proj, w_down, 1, 1) * D ** (-0.5)
    gradient = gradient + through - row_dot * wide_rows / (D * root_mean * root_mean)
    moment_down = moment_decay * moments[0] + grad_down
    moment_up = moment_decay * moments[1] + grad_up
    new_down = (w_down.astype(jnp.float32) - learn_rate * moment_down).astype(jnp.bfloat16)
    new_up = (w_up.astype(jnp.float32) - learn_rate * moment_up).astype(jnp.bfloat16)
    return (gradient, (new_down, new_up, moment_down, moment_up))


def average_whole(states):
    replicas = lax.axis_size("row")
    flat_down = states[0].astype(jnp.float32).reshape(-1)
    flat_up = states[1].astype(jnp.float32).reshape(-1)
    flat_mdown = states[2].reshape(-1)
    flat_mup = states[3].reshape(-1)
    totals = (
        lax.psum_scatter(flat_down, "row", scatter_dimension=0, tiled=True),
        lax.psum_scatter(flat_up, "row", scatter_dimension=0, tiled=True),
        lax.psum_scatter(flat_mdown, "row", scatter_dimension=0, tiled=True),
        lax.psum_scatter(flat_mup, "row", scatter_dimension=0, tiled=True),
    )
    share_down = (totals[0] / replicas).astype(jnp.bfloat16)
    share_up = (totals[1] / replicas).astype(jnp.bfloat16)
    params = (
        lax.all_gather(share_down, "row", axis=0, tiled=True),
        lax.all_gather(share_up, "row", axis=0, tiled=True),
    )
    moments = (
        lax.all_gather(
            (totals[2] / replicas).astype(jnp.bfloat16), "row", axis=0, tiled=True
        ).astype(jnp.float32),
        lax.all_gather(
            (totals[3] / replicas).astype(jnp.bfloat16), "row", axis=0, tiled=True
        ).astype(jnp.float32),
    )
    return (
        params[0].reshape(states[0].shape),
        params[1].reshape(states[1].shape),
        moments[0].reshape(states[2].shape),
        moments[1].reshape(states[3].shape),
    )


def body(hidden, target, w_down, w_up, m_down, m_up):
    tokens = hidden[0]
    target_rows = target[0].astype(jnp.float32)
    states = (w_down[0], w_up[0], m_down[0], m_up[0])
    for step_index in range(STEPS):
        outcome, stored = lax.scan(forward_layer, tokens, (states[0], states[1]))
        gradient = outcome.astype(jnp.float32) - target_rows
        gradient, states = lax.scan(
            backward_layer,
            gradient,
            (stored, (states[0], states[1]), (states[2], states[3])),
            reverse=True,
        )
    states = average_whole(states)
    return (states[0], states[1], states[2], states[3])


def solution(mesh):
    placed = (
        P("row", None, "ta"),
        P("row", None, "ta"),
        P("row", None, "ta", None),
        P("row", None, None, "ta"),
        P("row", None, "ta", None),
        P("row", None, None, "ta"),
    )
    return jax.shard_map(
        body,
        mesh=mesh,
        in_specs=placed,
        out_specs=(
            P(None, "ta", None),
            P(None, None, "ta"),
            P(None, "ta", None),
            P(None, None, "ta"),
        ),
        check_vma=False,
    )
```

profile of v0, /device:TPU:0, one launch (start us, length us, event | category | flops | bytes accessed | tf_op | source)
XLA Modules:
  0.0 1070.3 jit_solution(8603271068688036088)
XLA Ops:
  11.1 83.1 %while.160 = (s32[]{:T(128)}, bf16[256,896]{1,0:T(8,128)(2,1)S(1)}, bf16[2,256,896]{2,1,0:T(8,128)(2,1)}, f32[2,256,1]{1,2,0:T(1,128)S(1)}, f32[2,256,256]{1,2,0...) while((s32[]{:T(128)}, bf16[256,896]{1,0:T(8,128)(2,1)S(1)}, ...), condition=%wide.region_4.5_spmd, body=%wide.region_0.4_spmd.sunk | while | flops 237470208 | bytes 6695077 | solution.py:103
  14.2 8.3 psum.121
  22.6 27.2 %all-reduce.17.cloned.1.call-done = f32[256,256]{0,1:T(8,128)} async-done(((f32[256,256]{0,1:T(8,128)}), f32[256,256]{0,1:T(8,128)}) %all-reduce.17.cloned.1.call-update) | async-done | bytes 262160 | tf_op jit(solution)/shard_map/while/body/eval_jaxpr/psum | solution.py:32
  62.9 27.1 %all-reduce.17.cloned.1.call-done = f32[256,256]{0,1:T(8,128)} async-done(((f32[256,256]{0,1:T(8,128)}), f32[256,256]{0,1:T(8,128)}) %all-reduce.17.cloned.1.call-update) | async-done | bytes 262160 | tf_op jit(solution)/shard_map/while/body/eval_jaxpr/psum | solution.py:32
  98.1 80.0 %while.161 = (s32[]{:T(128)}, f32[256,896]{1,0:T(8,128)S(1)}, bf16[2,896,256]{2,1,0:T(8,128)(2,1)}, bf16[2,256,896]{2,1,0:T(8,128)(2,1)S(1)}, f32[2,896,256]{2,1...) while((s32[]{:T(128)}, f32[256,896]{1,0:T(8,128)S(1)}, ...), condition=%wide.region_8.9_spmd, body=%wide.region_5.8_spmd.sunk | while | flops 477167872 | bytes 56243636 | solution.py:105
  103.3 29.7 %all-reduce.19.cloned.1.call-done = bf16[256,256]{0,1:T(8,128)(2,1)} async-done(((bf16[256,256]{0,1:T(8,128)(2,1)}), bf16[256,256]{0,1:T(8,128)(2,1)}) %all-reduce.19.cloned.1.call-update) | async-done | bytes 131088 | tf_op jit(solution)/shard_map/while/body/eval_jaxpr/psum | solution.py:47
  143.5 29.3 %all-reduce.19.cloned.1.call-done = bf16[256,256]{0,1:T(8,128)(2,1)} async-done(((bf16[256,256]{0,1:T(8,128)(2,1)}), bf16[256,256]{0,1:T(8,128)(2,1)}) %all-reduce.19.cloned.1.call-update) | async-done | bytes 131088 | tf_op jit(solution)/shard_map/while/body/eval_jaxpr/psum | solution.py:47
  179.2 77.3 %while.162 = (s32[]{:T(128)}, bf16[256,896]{1,0:T(8,128)(2,1)S(1)}, bf16[2,256,896]{2,1,0:T(8,128)(2,1)}, f32[2,256,1]{1,2,0:T(1,128)S(1)}, f32[2,256,256]{1,2,0...) while((s32[]{:T(128)}, bf16[256,896]{1,0:T(8,128)(2,1)S(1)}, ...), condition=%wide.region_13.14_spmd, body=%wide.region_9.13_spmd.sunk | while | flops 237470208 | bytes 6695077 | solution.py:103
  182.3 5.7 psum.124
  188.1 26.3 %all-reduce.21.cloned.1.call-done = f32[256,256]{0,1:T(8,128)} async-done(((f32[256,256]{0,1:T(8,128)}), f32[256,256]{0,1:T(8,128)}) %all-reduce.21.cloned.1.call-update) | async-done | bytes 262160 | tf_op jit(solution)/shard_map/while/body/eval_jaxpr/psum | solution.py:32
  221.0 5.7 psum.124
  226.7 26.3 %all-reduce.21.cloned.1.call-done = f32[256,256]{0,1:T(8,128)} async-done(((f32[256,256]{0,1:T(8,128)}), f32[256,256]{0,1:T(8,128)}) %all-reduce.21.cloned.1.call-update) | async-done | bytes 262160 | tf_op jit(solution)/shard_map/while/body/eval_jaxpr/psum | solution.py:32
  263.1 80.4 %while.163 = (s32[]{:T(128)}, f32[256,896]{1,0:T(8,128)S(1)}, bf16[2,896,256]{2,1,0:T(8,128)(2,1)}, bf16[2,256,896]{2,1,0:T(8,128)(2,1)}, f32[2,896,256]{2,1,0:T...) while((s32[]{:T(128)}, f32[256,896]{1,0:T(8,128)S(1)}, ...), condition=%wide.region_17.18_spmd, body=%wide.region_14.17_spmd.sunk | while | flops 477167872 | bytes 56243636 | solution.py:105
  267.9 30.1 %all-reduce.23.cloned.1.call-done = bf16[256,256]{0,1:T(8,128)(2,1)} async-done(((bf16[256,256]{0,1:T(8,128)(2,1)}), bf16[256,256]{0,1:T(8,128)(2,1)}) %all-reduce.23.cloned.1.call-update) | async-done | bytes 131088 | tf_op jit(solution)/shard_map/while/body/eval_jaxpr/psum | solution.py:47
  308.1 30.1 %all-reduce.23.cloned.1.call-done = bf16[256,256]{0,1:T(8,128)(2,1)} async-done(((bf16[256,256]{0,1:T(8,128)(2,1)}), bf16[256,256]{0,1:T(8,128)(2,1)}) %all-reduce.23.cloned.1.call-update) | async-done | bytes 131088 | tf_op jit(solution)/shard_map/while/body/eval_jaxpr/psum | solution.py:47
  344.5 78.8 %while.164 = (s32[]{:T(128)}, bf16[256,896]{1,0:T(8,128)(2,1)S(1)}, bf16[2,256,896]{2,1,0:T(8,128)(2,1)}, f32[2,256,1]{1,2,0:T(1,128)S(1)}, f32[2,256,256]{1,2,0...) while((s32[]{:T(128)}, bf16[256,896]{1,0:T(8,128)(2,1)S(1)}, ...), condition=%wide.region_22.23_spmd, body=%wide.region_18.22_spmd.sunk | while | flops 237470208 | bytes 10365121 | solution.py:103
  353.5 27.0 %all-reduce.25.cloned.1.call-done = f32[256,256]{0,1:T(8,128)} async-done(((f32[256,256]{0,1:T(8,128)}), f32[256,256]{0,1:T(8,128)}) %all-reduce.25.cloned.1.call-update) | async-done | bytes 262160 | tf_op jit(solution)/shard_map/while/body/eval_jaxpr/psum | solution.py:32
  393.1 26.7 %all-reduce.25.cloned.1.call-done = f32[256,256]{0,1:T(8,128)} async-done(((f32[256,256]{0,1:T(8,128)}), f32[256,256]{0,1:T(8,128)}) %all-reduce.25.cloned.1.call-update) | async-done | bytes 262160 | tf_op jit(solution)/shard_map/while/body/eval_jaxpr/psum | solution.py:32
  428.8 80.1 %while.165 = (s32[]{:T(128)}, f32[256,896]{1,0:T(8,128)S(1)}, bf16[2,896,256]{2,1,0:T(8,128)(2,1)}, bf16[2,256,896]{2,1,0:T(8,128)(2,1)}, f32[2,896,256]{2,1,0:T...) while((s32[]{:T(128)}, f32[256,896]{1,0:T(8,128)S(1)}, ...), condition=%wide.region_26.27_spmd, body=%wide.region_23.26_spmd.sunk | while | flops 477167872 | bytes 56243636 | solution.py:105
  433.6 30.1 %all-reduce.27.cloned.1.call-done = bf16[256,256]{0,1:T(8,128)(2,1)} async-done(((bf16[256,256]{0,1:T(8,128)(2,1)}), bf16[256,256]{0,1:T(8,128)(2,1)}) %all-reduce.27.cloned.1.call-update) | async-done | bytes 131088 | tf_op jit(solution)/shard_map/while/body/eval_jaxpr/psum | solution.py:47
  473.8 29.8 %all-reduce.27.cloned.1.call-done = bf16[256,256]{0,1:T(8,128)(2,1)} async-done(((bf16[256,256]{0,1:T(8,128)(2,1)}), bf16[256,256]{0,1:T(8,128)(2,1)}) %all-reduce.27.cloned.1.call-update) | async-done | bytes 131088 | tf_op jit(solution)/shard_map/while/body/eval_jaxpr/psum | solution.py:47
  509.9 77.6 %while.166 = (s32[]{:T(128)}, bf16[256,896]{1,0:T(8,128)(2,1)S(1)}, bf16[2,256,896]{2,1,0:T(8,128)(2,1)}, f32[2,256,1]{1,2,0:T(1,128)S(1)}, f32[2,256,256]{1,2,0...) while((s32[]{:T(128)}, bf16[256,896]{1,0:T(8,128)(2,1)S(1)}, ...), condition=%wide.region_31.32_spmd, body=%wide.region_27.31_spmd.sunk | while | flops 237470208 | bytes 10365121 | solution.py:103
  518.9 26.5 %all-reduce.29.cloned.1.call-done = f32[256,256]{0,1:T(8,128)} async-done(((f32[256,256]{0,1:T(8,128)}), f32[256,256]{0,1:T(8,128)}) %all-reduce.29.cloned.1.call-update) | async-done | bytes 262160 | tf_op jit(solution)/shard_map/while/body/eval_jaxpr/psum | solution.py:32
  557.8 26.2 %all-reduce.29.cloned.1.call-done = f32[256,256]{0,1:T(8,128)} async-done(((f32[256,256]{0,1:T(8,128)}), f32[256,256]{0,1:T(8,128)}) %all-reduce.29.cloned.1.call-update) | async-done | bytes 262160 | tf_op jit(solution)/shard_map/while/body/eval_jaxpr/psum | solution.py:32
  593.0 80.6 %while.167 = (s32[]{:T(128)}, f32[256,896]{1,0:T(8,128)S(1)}, bf16[2,896,256]{2,1,0:T(8,128)(2,1)}, bf16[2,256,896]{2,1,0:T(8,128)(2,1)}, f32[2,896,256]{2,1,0:T...) while((s32[]{:T(128)}, f32[256,896]{1,0:T(8,128)S(1)}, ...), condition=%wide.region_35.36_spmd, body=%wide.region_32.35_spmd.sunk | while | flops 477167872 | bytes 52573592 | solution.py:105
  597.8 30.4 %all-reduce.31.cloned.1.call-done = bf16[256,256]{0,1:T(8,128)(2,1)} async-done(((bf16[256,256]{0,1:T(8,128)(2,1)}), bf16[256,256]{0,1:T(8,128)(2,1)}) %all-reduce.31.cloned.1.call-update) | async-done | bytes 131088 | tf_op jit(solution)/shard_map/while/body/eval_jaxpr/psum | solution.py:47
  638.1 30.4 %all-reduce.31.cloned.1.call-done = bf16[256,256]{0,1:T(8,128)(2,1)} async-done(((bf16[256,256]{0,1:T(8,128)(2,1)}), bf16[256,256]{0,1:T(8,128)(2,1)}) %all-reduce.31.cloned.1.call-update) | async-done | bytes 131088 | tf_op jit(solution)/shard_map/while/body/eval_jaxpr/psum | solution.py:47
  685.9 237.4 %all-reduce.15.cloned.1.call-done = (f32[458752]{0:T(1024)}, f32[458752]{0:T(1024)}, f32[458752]{0:T(1024)}, f32[458752]{0:T(1024)}) async-done(((f32[458752]{0:T(1024)}, f32[458752]{0:T(1024)}, f32[458752]{0:T(1024)}, f32[458752]{0:T(1024)}), (f32[458752]{0:T(1024)}, f32[458752]{0:T(1024)}, f32[458752]{0:T(1024)}, f32[458752]{0:T(1024)})) %all-reduce.15.cloned.1.call-update) | async-done | bytes 7340048
  924.3 32.4 %all_gather.14 = bf16[458752]{0:T(1024)(128)(2,1)S(1)} all-gather(bf16[57344]{0:T(1024)(128)(2,1)S(1)} %fusion.173), channel_id=1, replica_groups=mesh['row'=8,'ta'=4] {'row'}, dimensions={0}, use_global_device_ids=true | all-gather | bytes 1032192 | tf_op jit(solution)/shard_map/all_gather | solution.py:83
  959.1 32.4 %all_gather.15 = bf16[458752]{0:T(1024)(128)(2,1)S(1)} all-gather(bf16[57344]{0:T(1024)(128)(2,1)S(1)} %fusion.172), channel_id=1, replica_groups=mesh['row'=8,'ta'=4] {'row'}, dimensions={0}, use_global_device_ids=true | all-gather | bytes 1032192 | tf_op jit(solution)/shard_map/all_gather | solution.py:86
  994.5 32.7 %all_gather.12 = bf16[458752]{0:T(1024)(128)(2,1)S(1)} all-gather(bf16[57344]{0:T(1024)(128)(2,1)S(1)} %fusion.175), channel_id=1, replica_groups=mesh['row'=8,'ta'=4] {'row'}, dimensions={0}, use_global_device_ids=true | all-gather | bytes 1032192 | tf_op jit(solution)/shard_map/all_gather | solution.py:79
  1029.5 31.9 %all_gather.13 = bf16[458752]{0:T(1024)(128)(2,1)S(1)} all-gather(bf16[57344]{0:T(1024)(128)(2,1)S(1)} %fusion.174), channel_id=1, replica_groups=mesh['row'=8,'ta'=4] {'row'}, dimensions={0}, use_global_device_ids=true | all-gather | bytes 1032192 | tf_op jit(solution)/shard_map/all_gather | solution.py:80
  (385 shorter events, 213.5 us)
Async XLA Ops:
  11.0 83.2 %copy-start.14 = (bf16[1,256,896]{2,1,0:T(8,128)(2,1)S(1)}, bf16[1,256,896]{2,1,0:T(8,128)(2,1)}, u32[]{:S(2)}) copy-start(bf16[1,256,896]{2,1,0:T(8,128)(2,1)} %param.23) | copy-start | bytes 1376260
  11.1 38.7 %all-reduce.17.cloned.1.call-start = ((), (), s32[]{:S(2)}) async-start(), calls=%async_computation.1 | async-start | bytes 524288 | tf_op jit(solution)/shard_map/while/body/eval_jaxpr/psum | solution.py:32
  54.0 36.0 %all-reduce.17.cloned.1.call-start = ((), (), s32[]{:S(2)}) async-start(), calls=%async_computation.1 | async-start | bytes 524288 | tf_op jit(solution)/shard_map/while/body/eval_jaxpr/psum | solution.py:32
  98.1 34.9 %all-reduce.19.cloned.1.call-start = ((), (), s32[]{:S(2)}) async-start(), calls=%async_computation.2 | async-start | bytes 262144 | tf_op jit(solution)/shard_map/while/body/eval_jaxpr/psum | solution.py:47
  133.0 4.2 copy-start.40
  138.3 34.6 %all-reduce.19.cloned.1.call-start = ((), (), s32[]{:S(2)}) async-start(), calls=%async_computation.2 | async-start | bytes 262144 | tf_op jit(solution)/shard_map/while/body/eval_jaxpr/psum | solution.py:47
  172.9 4.2 copy-start.40
  179.2 35.1 %all-reduce.21.cloned.1.call-start = ((), (), s32[]{:S(2)}) async-start(), calls=%async_computation.3 | async-start | bytes 524288 | tf_op jit(solution)/shard_map/while/body/eval_jaxpr/psum | solution.py:32
  217.8 35.1 %all-reduce.21.cloned.1.call-start = ((), (), s32[]{:S(2)}) async-start(), calls=%async_computation.3 | async-start | bytes 524288 | tf_op jit(solution)/shard_map/while/body/eval_jaxpr/psum | solution.py:32
  263.1 34.9 %all-reduce.23.cloned.1.call-start = ((), (), s32[]{:S(2)}) async-start(), calls=%async_computation.4 | async-start | bytes 262144 | tf_op jit(solution)/shard_map/while/body/eval_jaxpr/psum | solution.py:47
  298.0 4.2 copy-start.41
  303.3 34.9 %all-reduce.23.cloned.1.call-start = ((), (), s32[]{:S(2)}) async-start(), calls=%async_computation.4 | async-start | bytes 262144 | tf_op jit(solution)/shard_map/while/body/eval_jaxpr/psum | solution.py:47
  338.2 4.2 copy-start.41
  344.5 78.8 %copy-start.15 = (bf16[1,256,896]{2,1,0:T(8,128)(2,1)S(1)}, bf16[1,256,896]{2,1,0:T(8,128)(2,1)}, u32[]{:S(2)}) copy-start(bf16[1,256,896]{2,1,0:T(8,128)(2,1)} %param.23) | copy-start | bytes 1376260
  344.6 36.0 %all-reduce.25.cloned.1.call-start = ((), (), s32[]{:S(2)}) async-start(), calls=%async_computation.5 | async-start | bytes 524288 | tf_op jit(solution)/shard_map/while/body/eval_jaxpr/psum | solution.py:32
  344.6 38.0 %copy-start = (bf16[2,256,896]{2,1,0:T(8,128)(2,1)S(1)}, bf16[2,256,896]{2,1,0:T(8,128)(2,1)}, u32[]{:S(2)}) copy-start(bf16[2,256,896]{2,1,0:T(8,128)(2,1)} %get-tuple-element.2377) | copy-start | bytes 2752516 | tf_op jit(solution)/shard_map/while
  384.1 35.7 %all-reduce.25.cloned.1.call-start = ((), (), s32[]{:S(2)}) async-start(), calls=%async_computation.5 | async-start | bytes 524288 | tf_op jit(solution)/shard_map/while/body/eval_jaxpr/psum | solution.py:32
  384.1 37.7 %copy-start = (bf16[2,256,896]{2,1,0:T(8,128)(2,1)S(1)}, bf16[2,256,896]{2,1,0:T(8,128)(2,1)}, u32[]{:S(2)}) copy-start(bf16[2,256,896]{2,1,0:T(8,128)(2,1)} %get-tuple-element.2377) | copy-start | bytes 2752516 | tf_op jit(solution)/shard_map/while
  425.4 3.3 copy-start.1
  428.8 34.9 %all-reduce.27.cloned.1.call-start = ((), (), s32[]{:S(2)}) async-start(), calls=%async_computation.6 | async-start | bytes 262144 | tf_op jit(solution)/shard_map/while/body/eval_jaxpr/psum | solution.py:47
  463.7 4.2 copy-start.42
  469.0 34.6 %all-reduce.27.cloned.1.call-start = ((), (), s32[]{:S(2)}) async-start(), calls=%async_computation.6 | async-start | bytes 262144 | tf_op jit(solution)/shard_map/while/body/eval_jaxpr/psum | solution.py:47
  503.6 4.2 copy-start.42
  509.9 35.5 %all-reduce.29.cloned.1.call-start = ((), (), s32[]{:S(2)}) async-start(), calls=%async_computation.7 | async-start | bytes 524288 | tf_op jit(solution)/shard_map/while/body/eval_jaxpr/psum | solution.py:32
  510.0 37.4 %copy-start.2 = (bf16[2,256,896]{2,1,0:T(8,128)(2,1)S(1)}, bf16[2,256,896]{2,1,0:T(8,128)(2,1)}, u32[]{:S(2)}) copy-start(bf16[2,256,896]{2,1,0:T(8,128)(2,1)} %get-tuple-element.2449) | copy-start | bytes 2752516 | tf_op jit(solution)/shard_map/while
  548.9 35.1 %all-reduce.29.cloned.1.call-start = ((), (), s32[]{:S(2)}) async-start(), calls=%async_computation.7 | async-start | bytes 524288 | tf_op jit(solution)/shard_map/while/body/eval_jaxpr/psum | solution.py:32
  548.9 37.1 %copy-start.2 = (bf16[2,256,896]{2,1,0:T(8,128)(2,1)S(1)}, bf16[2,256,896]{2,1,0:T(8,128)(2,1)}, u32[]{:S(2)}) copy-start(bf16[2,256,896]{2,1,0:T(8,128)(2,1)} %get-tuple-element.2449) | copy-start | bytes 2752516 | tf_op jit(solution)/shard_map/while
  589.7 3.3 copy-start.3
  589.7 3.3 copy-start.13
  593.0 35.2 %all-reduce.31.cloned.1.call-start = ((), (), s32[]{:S(2)}) async-start(), calls=%async_computation.8 | async-start | bytes 262144 | tf_op jit(solution)/shard_map/while/body/eval_jaxpr/psum | solution.py:47
  633.3 35.2 %all-reduce.31.cloned.1.call-start = ((), (), s32[]{:S(2)}) async-start(), calls=%async_computation.8 | async-start | bytes 262144 | tf_op jit(solution)/shard_map/while/body/eval_jaxpr/psum | solution.py:47
  673.6 249.7 %all-reduce.15.cloned.1.call-start = ((), (), s32[]{:S(2)}) async-start(), calls=%async_computation | async-start | bytes 14680064
  (63 other events, 99.5 us)
Sparse Core Ops, SparseCore 0:
  14.8 34.9 all-reduce.16
  57.7 32.2 all-reduce.16
  101.2 31.7 all-reduce.18
  141.1 31.7 all-reduce.18
  182.0 32.2 all-reduce.20
  220.7 32.2 all-reduce.20
  266.2 31.7 all-reduce.22
  306.4 31.7 all-reduce.22
  348.3 32.2 all-reduce.24
  387.5 32.2 all-reduce.24
  431.9 31.7 all-reduce.26
  471.7 31.7 all-reduce.26
  513.1 32.2 all-reduce.28
  551.7 32.2 all-reduce.28
  596.4 31.7 all-reduce.30
  636.7 31.7 all-reduce.30
Sparse Core Ops, SparseCore 1:
  684.2 239.1 all-reduce.14
where the time goes:
time: 1070 us
  waiting for transfers between devices  691 us (65%)
  blocking collectives  178 us (17%)
  matrix products  85.7 us (8%)
  local copies, waits for them, and re-layouts  72.1 us (7%)
  other arithmetic  26.6 us (2%)
  between operations  16.1 us (2%)
    psum x8, waiting for transfers between devices, backward_layer(): lax.psum((contract(grad_low, w_up, 1, 1) * RANK ** (-0.5)).astype(jnp.bfl...  240 us
    unnamed x2, waiting for transfers between devices  237 us
    psum x8, waiting for transfers between devices, forward_layer(): projected, total_sq = lax.psum((partial_value, squares), 'ta')  213 us
    dot_general x32, matrix products, contract(): lax.dot_general(matrix_a, matrix_b, (((dim_a,), (dim_b,)), ((), ())), pre...  57 us
    psum x8, blocking collectives, forward_layer(): projected, total_sq = lax.psum((partial_value, squares), 'ta')  48.4 us
    all_gather x1, blocking collectives, average_whole(): lax.all_gather(share_down, 'row', axis=0, tiled=True)  32.7 us
    all_gather x1, blocking collectives, average_whole(): lax.all_gather((totals[2] / replicas).astype(jnp.bfloat16), 'row', axis=0...  32.4 us
    all_gather x1, blocking collectives, average_whole(): lax.all_gather((totals[3] / replicas).astype(jnp.bfloat16), 'row', axis=0...  32.4 us
  transfers between devices with their start and end apart: 17, of which 17 were waited for; matrix products, arithmetic and copies ran while one was open for 3% of the time, Pallas kernels for 0%

commit v1 on v0

v1 whole, which is shorter than its diff:
```python
import functools

import jax
import jax.numpy as jnp
from jax import lax
from jax.experimental import pallas as pl
from jax.experimental.pallas import tpu as pltpu
from jax.sharding import PartitionSpec as P

MESH = pl.DeviceIdType.MESH
STEPS = 4
norm_eps = 1e-06
learn_rate = 0.02
moment_decay = 0.9


def dot_nn(a, b):
    return jnp.dot(a, b, preferred_element_type=jnp.float32)


def dot_nt(a, b):
    return lax.dot_general(a, b, (((1,), (1,)), ((), ())), preferred_element_type=jnp.float32)


def local_kernel(
    shards,
    x0_ref, tg_ref, wd_in, wu_in, md_in, mu_in,
    wd, wu, md_out, mu_out,
    md, mu, x1, xt, gr, pre, act, inv, tot, sqs, low,
    s1, r1, s2, r2, s3, r3, q1, p1, q2, p2, q3, p3,
    main_send, main_recv, side_send, side_recv,
):
    tok, width = x0_ref.shape
    rank = wd.shape[2]
    full = width * shards
    half = tok // 2
    chips = shards // 2
    me = lax.axis_index("ta")
    core = lax.rem(me, 2)
    sibling = me + 1 - 2 * core
    partners = [lax.rem(me + 2 * k, shards) for k in range(1, chips)]
    d_scale = full ** (-0.5)
    r_scale = rank ** (-0.5)

    barrier = pltpu.get_barrier_semaphore()
    for peer in [sibling] + partners:
        pl.semaphore_signal(barrier, inc=1, device_id={"ta": peer}, device_id_type=MESH)
    pl.semaphore_wait(barrier, chips)

    wd[...] = wd_in[...]
    wu[...] = wu_in[...]
    md[...] = md_in[...]
    mu[...] = mu_in[...]

    mine = pl.ds(pl.multiple_of(core * half, half), half)
    other = pl.ds(pl.multiple_of((1 - core) * half, half), half)

    def send(src, dst, sems, index, peer):
        copy = pltpu.make_async_remote_copy(
            src_ref=src, dst_ref=dst,
            send_sem=sems[0].at[index], recv_sem=sems[1].at[index],
            device_id={"ta": peer}, device_id_type=MESH,
        )
        copy.start()
        return copy

    main = (main_send, main_recv)
    side = (side_send, side_recv)

    def to_row(column):
        return jnp.broadcast_to(column, (half, half)).T[0:8]

    def to_column(row):
        return jnp.broadcast_to(row[0:1, :], (half, half)).T[:, 0:1]

    def exchange(parity, value, squares, work):
        tot[...] = value
        s1[...] = tot[other, :].astype(jnp.bfloat16)
        copies = [send(s1, r1, main, 0, sibling)]
        if squares is not None:
            sqs[...] = squares
            q1[...] = to_row(sqs[other, :])
            copies.append(send(q1, p1, side, 0, sibling))
            own_row = to_row(sqs[mine, :])
        for copy in copies:
            copy.wait()
        pair = tot[mine, :] + r1[...].astype(jnp.float32)
        s2[...] = pair.astype(jnp.bfloat16)
        base = parity * (chips - 1)
        copies = [
            send(s2, r2.at[base + k], main, 1 + base + k, peer) for k, peer in enumerate(partners)
        ]
        if squares is not None:
            pair_row = own_row + p1[...]
            q2[...] = pair_row
            copies += [
                send(q2, p2.at[base + k], side, 1 + base + k, peer)
                for k, peer in enumerate(partners)
            ]
        if work is not None:
            work()
        for copy in copies:
            copy.wait()
        total = pair
        for k in range(chips - 1):
            total = total + r2[base + k].astype(jnp.float32)
        last = 1 + 2 * (chips - 1)
        s3[...] = total.astype(jnp.bfloat16)
        copies = [send(s3, r3, main, last, sibling)]
        tot[mine, :] = total
        if squares is not None:
            row = pair_row
            for k in range(chips - 1):
                row = row + p2[base + k]
            q3[...] = row
            copies.append(send(q3, p3, side, last, sibling))
            sqs[mine, :] = to_column(row)
        for copy in copies:
            copy.wait()
        tot[other, :] = r3[...].astype(jnp.float32)
        if squares is not None:
            sqs[other, :] = to_column(p3[...])

    def forward(layer, rows, wide_rows):
        squares = jnp.sum(wide_rows * wide_rows, axis=1, keepdims=True)
        exchange(layer, dot_nn(rows, wd[layer]) * d_scale, squares, None)
        inverse = lax.rsqrt(sqs[...] / full + norm_eps)
        preact = tot[...] * inverse
        activation = (preact * jax.nn.sigmoid(preact)).astype(jnp.bfloat16)
        inv[layer] = inverse
        pre[layer] = preact
        act[layer] = activation
        lifted = dot_nn(activation, wu[layer]) * r_scale
        return (wide_rows + lifted).astype(jnp.bfloat16)

    def update(w, m, layer, grad):
        moment = moment_decay * m[layer] + grad
        m[layer] = moment
        w[layer] = (w[layer].astype(jnp.float32) - learn_rate * moment).astype(jnp.bfloat16)

    def update_up(layer):
        update(wu, mu, layer, dot_nn(act[layer].T, gr[...].astype(jnp.bfloat16)) * r_scale)

    def low_grads(layer):
        preact = pre[layer]
        sig = jax.nn.sigmoid(preact)
        grad_pre = tot[...] * (sig * (1.0 + preact * (1.0 - sig)))
        low[...] = (grad_pre * inv[layer]).astype(jnp.bfloat16)
        return jnp.sum(grad_pre * preact, axis=1, keepdims=True)

    def step(index, carry):
        x1[...] = forward(0, x0_ref[...], x0_ref[...].astype(jnp.float32))
        outcome = forward(1, x1[...], x1[...].astype(jnp.float32))
        gr[...] = outcome.astype(jnp.float32) - tg_ref[...].astype(jnp.float32)

        partial_act = dot_nt(gr[...].astype(jnp.bfloat16), wu[1]) * r_scale
        exchange(0, partial_act, None, lambda: update_up(1))
        row_dot = low_grads(1)
        through = dot_nt(low[...], wd[1]) * d_scale
        coefficient = row_dot * inv[1] * inv[1] / full
        gr[...] = gr[...] + through - coefficient * x1[...].astype(jnp.float32)

        def work():
            update(wd, md, 1, dot_nn(x1[...].T, low[...]) * d_scale)
            update_up(0)

        partial_act = dot_nt(gr[...].astype(jnp.bfloat16), wu[0]) * r_scale
        exchange(1, partial_act, None, work)
        low_grads(0)
        update(wd, md, 0, dot_nn(xt[...], low[...]) * d_scale)
        return carry

    xt[...] = x0_ref[...].T
    lax.fori_loop(0, STEPS, step, 0)
    md_out[...] = md[...].astype(jnp.bfloat16)
    mu_out[...] = mu[...].astype(jnp.bfloat16)


def local_steps(shards, hidden, target, w_down, w_up, m_down, m_up):
    tok, width = hidden.shape
    layers, _, rank = w_down.shape
    half = tok // 2
    hops = shards // 2 - 1
    bf, f32 = jnp.bfloat16, jnp.float32
    vmem = pl.BlockSpec(memory_space=pltpu.VMEM)
    sems = 2 + 2 * hops
    return pl.pallas_call(
        functools.partial(local_kernel, shards),
        out_shape=[
            jax.ShapeDtypeStruct(w_down.shape, bf),
            jax.ShapeDtypeStruct(w_up.shape, bf),
            jax.ShapeDtypeStruct(m_down.shape, bf),
            jax.ShapeDtypeStruct(m_up.shape, bf),
        ],
        in_specs=[vmem] * 6,
        out_specs=[vmem] * 4,
        scratch_shapes=[
            pltpu.VMEM(m_down.shape, f32),
            pltpu.VMEM(m_up.shape, f32),
            pltpu.VMEM((tok, width), bf),
            pltpu.VMEM((width, tok), bf),
            pltpu.VMEM((tok, width), f32),
            pltpu.VMEM((layers, tok, rank), f32),
            pltpu.VMEM((layers, tok, rank), bf),
            pltpu.VMEM((layers, tok, 1), f32),
            pltpu.VMEM((tok, rank), f32),
            pltpu.VMEM((tok, 1), f32),
            pltpu.VMEM((tok, rank), bf),
            pltpu.VMEM((half, rank), bf),
            pltpu.VMEM((half, rank), bf),
            pltpu.VMEM((half, rank), bf),
            pltpu.VMEM((2 * hops, half, rank), bf),
            pltpu.VMEM((half, rank), bf),
            pltpu.VMEM((half, rank), bf),
            pltpu.VMEM((8, half), f32),
            pltpu.VMEM((8, half), f32),
            pltpu.VMEM((8, half), f32),
            pltpu.VMEM((2 * hops, 8, half), f32),
            pltpu.VMEM((8, half), f32),
            pltpu.VMEM((8, half), f32),
            pltpu.SemaphoreType.DMA((sems,)),
            pltpu.SemaphoreType.DMA((sems,)),
            pltpu.SemaphoreType.DMA((sems,)),
            pltpu.SemaphoreType.DMA((sems,)),
        ],
        compiler_params=pltpu.CompilerParams(
            collective_id=0, has_side_effects=True, vmem_limit_bytes=60 * 1024 * 1024
        ),
    )(hidden, target, w_down, w_up, m_down, m_up)


def body(shards, replicas, hidden, target, w_down, w_up, m_down, m_up):
    states = local_steps(
        shards, hidden[0], target[0], w_down[0], w_up[0], m_down[0], m_up[0]
    )
    totals = lax.psum(tuple(states), "row")
    scale = 1.0 / replicas
    means = [total.astype(jnp.float32) * scale for total in totals]
    return (
        means[0].astype(jnp.bfloat16),
        means[1].astype(jnp.bfloat16),
        means[2],
        means[3],
    )


def solution(mesh):
    placed = (
        P("row", None, "ta"),
        P("row", None, "ta"),
        P("row", None, "ta", None),
        P("row", None, None, "ta"),
        P("row", None, "ta", None),
        P("row", None, None, "ta"),
    )
    return jax.shard_map(
        functools.partial(body, mesh.shape["ta"], mesh.shape["row"]),
        mesh=mesh,
        in_specs=placed,
        out_specs=(
            P(None, "ta", None),
            P(None, None, "ta"),
            P(None, "ta", None),
            P(None, None, "ta"),
        ),
        check_vma=False,
    )
```

time: 1070 us -> 272 us (0.25)
  waiting for transfers between devices: 691 us -> 143 us
  blocking collectives: 178 us -> 0 us
  Pallas kernels: 0 us -> 110 us
  matrix products: 85.7 us -> 0 us
  local copies, waits for them, and re-layouts: 72.1 us -> 0.01 us
  other arithmetic: 26.6 us -> 5.21 us
    psum x16 -> x1, waiting for transfers between devices: 453 us -> 143 us  [body(): totals = lax.psum(tuple(states), 'row')]
    unnamed x2 -> x1, waiting for transfers between devices: 237 us -> 0.02 us
    all_gather x4 -> x0, blocking collectives: 129 us -> none  [the longest x1 32.7 us: average_whole(): lax.all_gather(share_down, 'row', axis=0, tiled=True)]
    pallas_call x0 -> x1, Pallas kernels: none -> 110 us  [local_steps(): pl.pallas_call(functools.partial(local_kernel, shards), out_shape=[jax.Sh...]
    dot_general x48 -> x0, matrix products: 85.7 us -> none  [the longest x32 57 us: contract(): lax.dot_general(matrix_a, matrix_b, (((dim_a,), (dim_b,)), ((), ())), pre...]
    psum x8 -> x0, blocking collectives: 48.4 us -> none  [forward_layer(): projected, total_sq = lax.psum((partial_value, squares), 'ta')]
    another operation x32 -> x0, local copies, waits for them, and re-layouts: 22.8 us -> none
    while x132 -> x0, local copies, waits for them, and re-layouts: 21.4 us -> none
  transfers between devices with their start and end apart: 17 -> 1, of which waited for: 17 -> 1; matrix products, arithmetic and copies ran while one was open for 3% -> 0% of each run, Pallas kernels for 0% -> 0%
where the time goes in v1:
time: 272 us
  waiting for transfers between devices  143 us (53%)
  Pallas kernels  110 us (40%)
  between operations  14 us (5%)
  other arithmetic  5.21 us (2%)
    psum x1, waiting for transfers between devices, body(): totals = lax.psum(tuple(states), 'row')  143 us
    pallas_call x1, Pallas kernels, local_steps(): pl.pallas_call(functools.partial(local_kernel, shards), out_shape=[jax.Sh...  110 us
  transfers between devices with their start and end apart: 1, of which 1 were waited for; matrix products, arithmetic and copies ran while one was open for 0% of the time, Pallas kernels for 0%

profile of v1, /device:TPU:0, one launch (start us, length us, event | category | flops | bytes accessed | tf_op | source)
XLA Modules:
  0.0 272.2 jit_solution(5048515148418939561)
XLA Ops:
  7.2 0.0 all-reduce.3.cloned.1.call-start
  7.2 109.6 %shard_map.93 = (bf16[2,896,256]{2,1,0:T(8,128)(2,1)}, bf16[2,256,896]{2,1,0:T(8,128)(2,1)}, bf16[2,896,256]{2,1,0:T(8,128)(2,1)}, bf16[2,256,896]{2,1,0:T(8,128)(2,1)}) custom-call(bf16[256,896]{1,0:T(8,128)(2,1)} %bitcast.10, bf16[256,896]{1,0:T(8,128)(2,1)} %bitcast.11, bf16[2,896,256]{2,1,0:T(8,128)(2,1)} %bitcast.8, bf16[2,256,896]{2,1,0:T(8,128)(2,1)} %bitcast.9, ...), custom_call_target="tpu_custom_call" | custom-call | tf_op jit(solution)/shard_map/pallas_call | solution.py:187
  116.8 0.0 all-reduce.3.cloned.1.call-update
  116.9 143.2 %all-reduce.3.cloned.1.call-done = (bf16[2,896,256]{2,1,0:T(8,128)(2,1)}, bf16[2,256,896]{2,1,0:T(8,128)(2,1)}, bf16[2,896,256]{2,1,0:T(8,128)(2,1)}, bf16[2,256,896]{2,1,0:T(8,128)(2,1)}) async-done(((bf16[2,896,256]{2,1,0:T(8,128)(2,1)}, bf16[2,256,896]{2,1,0:T(8,128)(2,1)}, bf16[2,896,256]{2,1,0:T(8,128)(2,1)}, bf16[2,256,896]{2,1,0:T(8,128)(2,1)}), (bf16[2,896,256]{2,1,0:T(8,128)(2,1)}, ...) | async-done | bytes 3670032 | tf_op jit(solution)/shard_map/psum | solution.py:236
  260.1 0.0 copy-start
  260.1 0.0 copy-start.1
  260.1 3.4 %convert_multiply_fusion.1 = (f32[2,896,256]{2,1,0:T(8,128)}, bf16[2,896,256]{2,1,0:T(8,128)(2,1)}) fusion(bf16[2,896,256]{2,1,0:T(8,128)(2,1)} %get-tuple-element.14, bf16[2,896,256]{2,1,0:T(8,128)(2,1)} %get-tuple-element.12), kind=kLoop, calls=%fused_computation.1 | loop fusion | flops 2293760 | bytes 4587520 | tf_op jit(solution)/shard_map/mul | solution.py:238
  263.5 0.0 copy-done
  263.5 0.0 copy-done.1
  263.5 1.8 convert_multiply_fusion
Async XLA Ops:
  7.2 252.9 %all-reduce.3.cloned.1.call-start = ((), (), s32[]{:S(2)}) async-start(), calls=%async_computation | async-start | bytes 7340032 | tf_op jit(solution)/shard_map/psum | solution.py:236
  260.1 3.4 %copy-start = (bf16[2,256,896]{2,1,0:T(8,128)(2,1)S(1)}, bf16[2,256,896]{2,1,0:T(8,128)(2,1)}, u32[]{:S(2)}) copy-start(bf16[2,256,896]{2,1,0:T(8,128)(2,1)} %get-tuple-element.13) | copy-start | bytes 2752516
  260.1 3.4 %copy-start.1 = (bf16[2,256,896]{2,1,0:T(8,128)(2,1)S(1)}, bf16[2,256,896]{2,1,0:T(8,128)(2,1)}, u32[]{:S(2)}) copy-start(bf16[2,256,896]{2,1,0:T(8,128)(2,1)} %get-tuple-element.15) | copy-start | bytes 2752516
Sparse Core Ops, SparseCore 0:
  117.0 143.0 all-reduce.2

commit v2 on v1

--- a/solution.py
+++ b/solution.py
@@ -22,11 +22,19 @@
     return lax.dot_general(a, b, (((1,), (1,)), ((), ())), preferred_element_type=jnp.float32)
 
 
-def local_kernel(
-    shards,
+def row_bits(replicas, *lengths):
+    if replicas & (replicas - 1) or any(length % (16 * replicas) for length in lengths):
+        return []
+    return [2**k for k in range(replicas.bit_length() - 1)]
+
+
+def fused_kernel(
+    shards, replicas,
     x0_ref, tg_ref, wd_in, wu_in, md_in, mu_in,
-    wd, wu, md_out, mu_out,
-    md, mu, x1, xt, gr, pre, act, inv, tot, sqs, low,
+    wd_out, wu_out, md_out, mu_out,
+    wd, wu, md, mu, mdl, mul, res_wd, res_wu, res_md, res_mu,
+    got_wd, got_wu, got_md, got_mu, row_send, row_recv,
+    x1, xt, gr, pre, act, inv, tot, sqs, low,
     s1, r1, s2, r2, s3, r3, q1, p1, q2, p2, q3, p3,
     main_send, main_recv, side_send, side_recv,
 ):
@@ -45,7 +53,14 @@
     barrier = pltpu.get_barrier_semaphore()
     for peer in [sibling] + partners:
         pl.semaphore_signal(barrier, inc=1, device_id={"ta": peer}, device_id_type=MESH)
-    pl.semaphore_wait(barrier, chips)
+    bits = row_bits(replicas, width, rank)
+    levels = len(bits)
+    spot = lax.axis_index("row")
+    own_bit = {bit: lax.rem(spot // bit, 2) for bit in bits}
+    row_peer = {bit: spot + bit - 2 * bit * own_bit[bit] for bit in bits}
+    for bit in bits:
+        pl.semaphore_signal(barrier, inc=1, device_id={"row": row_peer[bit]}, device_id_type=MESH)
+    pl.semaphore_wait(barrier, chips + levels)
 
     wd[...] = wd_in[...]
     wu[...] = wu_in[...]
@@ -148,6 +163,47 @@
         low[...] = (grad_pre * inv[layer]).astype(jnp.bfloat16)
         return jnp.sum(grad_pre * preact, axis=1, keepdims=True)
 
+    plain = list(bits)
+    swapped = plain[:2][::-1] + plain[2:]
+    down, up = (wd, got_wd, res_wd), (wu, got_wu, res_wu)
+    mdown, mup = (mdl, got_md, res_md), (mul, got_mu, res_mu)
+    chunks = []
+    for layer in reversed(range(wd.shape[0])):
+        for group in ((up, mup), (down, mdown)):
+            for triple in group:
+                order = swapped if len(chunks) in (1, 4) else plain
+                chunks.append(triple + (layer, order))
+    late = [k for k, entry in enumerate(chunks) if entry[3] == 0 and (entry[0] is wd or entry[0] is mdl)]
+    early = [k for k in range(len(chunks)) if k not in late]
+
+    def region(chunk, depth):
+        acc, _, _, _, order = chunks[chunk]
+        start = 0
+        for k in range(depth):
+            start = start + own_bit[order[k]] * (acc.shape[1] >> (k + 1))
+        return pl.multiple_of(start, acc.shape[1] >> depth) if depth else 0
+
+    def row_copy(chunk, stage):
+        acc, got, res, layer, order = chunks[chunk]
+        rows = acc.shape[1]
+        if stage < levels:
+            bit = order[stage]
+            size = rows >> (stage + 1)
+            away = region(chunk, stage) + (1 - own_bit[bit]) * size
+            src = acc.at[layer, pl.ds(pl.multiple_of(away, size), size)]
+            dst = got.at[layer, pl.ds(rows - 2 * size, size)]
+        else:
+            depth = 2 * levels - stage
+            bit = order[depth - 1]
+            part = pl.ds(region(chunk, depth), rows >> depth)
+            src = dst = res.at[layer, part]
+        index = chunk * 2 * levels + stage
+        return pltpu.make_async_remote_copy(
+            src_ref=src, dst_ref=dst,
+            send_sem=row_send.at[index], recv_sem=row_recv.at[index],
+            device_id={"row": row_peer[bit]}, device_id_type=MESH,
+        )
+
     def step(index, carry):
         x1[...] = forward(0, x0_ref[...], x0_ref[...].astype(jnp.float32))
         outcome = forward(1, x1[...], x1[...].astype(jnp.float32))
@@ -164,6 +220,13 @@
             update(wd, md, 1, dot_nn(x1[...].T, low[...]) * d_scale)
             update_up(0)
 
+            @pl.when(index == STEPS - 1)
+            def _():
+                mul[...] = mu[...].astype(jnp.bfloat16)
+                mdl[1] = md[1].astype(jnp.bfloat16)
+                for chunk in early if levels else []:
+                    row_copy(chunk, 0).start()
+
         partial_act = dot_nt(gr[...].astype(jnp.bfloat16), wu[0]) * r_scale
         exchange(1, partial_act, None, work)
         low_grads(0)
@@ -172,11 +235,45 @@
 
     xt[...] = x0_ref[...].T
     lax.fori_loop(0, STEPS, step, 0)
-    md_out[...] = md[...].astype(jnp.bfloat16)
-    mu_out[...] = mu[...].astype(jnp.bfloat16)
-
-
-def local_steps(shards, hidden, target, w_down, w_up, m_down, m_up):
+    mdl[0] = md[0].astype(jnp.bfloat16)
+    if not levels:
+        wd_out[...] = wd[...]
+        wu_out[...] = wu[...]
+        md_out[...] = mdl[...]
+        mu_out[...] = mul[...]
+        return
+    for chunk in late:
+        row_copy(chunk, 0).start()
+
+    count = len(chunks)
+    for slot in range(count + 2 * levels - 1):
+        for chunk in range(count):
+            stage = slot - chunk
+            if stage < 0 or stage >= 2 * levels:
+                continue
+            row_copy(chunk, stage).wait_recv()
+            if stage < levels:
+                acc, got, res, layer, order = chunks[chunk]
+                size = acc.shape[1] >> (stage + 1)
+                keep = pl.ds(region(chunk, stage + 1), size)
+                landed = got.at[layer, pl.ds(acc.shape[1] - 2 * size, size)]
+                total = acc[layer, keep, :].astype(jnp.float32) + landed[...].astype(jnp.float32)
+                if stage < levels - 1:
+                    acc[layer, keep, :] = total.astype(jnp.bfloat16)
+                else:
+                    res[layer, keep, :] = (total * (1.0 / replicas)).astype(jnp.bfloat16)
+            if stage < 2 * levels - 1:
+                row_copy(chunk, stage + 1).start()
+    for chunk in range(count):
+        for stage in range(2 * levels):
+            row_copy(chunk, stage).wait_send()
+    wd_out[...] = res_wd[...]
+    wu_out[...] = res_wu[...]
+    md_out[...] = res_md[...]
+    mu_out[...] = res_mu[...]
+
+
+def fused(shards, replicas, hidden, target, w_down, w_up, m_down, m_up):
     tok, width = hidden.shape
     layers, _, rank = w_down.shape
     half = tok // 2
@@ -184,8 +281,9 @@
     bf, f32 = jnp.bfloat16, jnp.float32
     vmem = pl.BlockSpec(memory_space=pltpu.VMEM)
     sems = 2 + 2 * hops
+    row_sems = max(1, 4 * layers * 2 * len(row_bits(replicas, width, rank)))
     return pl.pallas_call(
-        functools.partial(local_kernel, shards),
+        functools.partial(fused_kernel, shards, replicas),
         out_shape=[
             jax.ShapeDtypeStruct(w_down.shape, bf),
             jax.ShapeDtypeStruct(w_up.shape, bf),
@@ -195,8 +293,22 @@
         in_specs=[vmem] * 6,
         out_specs=[vmem] * 4,
         scratch_shapes=[
+            pltpu.VMEM(w_down.shape, bf),
+            pltpu.VMEM(w_up.shape, bf),
             pltpu.VMEM(m_down.shape, f32),
             pltpu.VMEM(m_up.shape, f32),
+            pltpu.VMEM(m_down.shape, bf),
+            pltpu.VMEM(m_up.shape, bf),
+            pltpu.VMEM(w_down.shape, bf),
+            pltpu.VMEM(w_up.shape, bf),
+            pltpu.VMEM(m_down.shape, bf),
+            pltpu.VMEM(m_up.shape, bf),
+            pltpu.VMEM(w_down.shape, bf),
+            pltpu.VMEM(w_up.shape, bf),
+            pltpu.VMEM(m_down.shape, bf),
+            pltpu.VMEM(m_up.shape, bf),
+            pltpu.SemaphoreType.DMA((row_sems,)),
+            pltpu.SemaphoreType.DMA((row_sems,)),
             pltpu.VMEM((tok, width), bf),
             pltpu.VMEM((width, tok), bf),
             pltpu.VMEM((tok, width), f32),
@@ -230,17 +342,17 @@
 
 
 def body(shards, replicas, hidden, target, w_down, w_up, m_down, m_up):
-    states = local_steps(
-        shards, hidden[0], target[0], w_down[0], w_up[0], m_down[0], m_up[0]
+    means = fused(
+        shards, replicas, hidden[0], target[0], w_down[0], w_up[0], m_down[0], m_up[0]
     )
-    totals = lax.psum(tuple(states), "row")
-    scale = 1.0 / replicas
-    means = [total.astype(jnp.float32) * scale for total in totals]
+    if not row_bits(replicas, hidden.shape[2], w_down.shape[3]):
+        totals = lax.psum(tuple(means), "row")
+        means = [total.astype(jnp.float32) / replicas for total in totals]
     return (
         means[0].astype(jnp.bfloat16),
         means[1].astype(jnp.bfloat16),
-        means[2],
-        means[3],
+        means[2].astype(jnp.float32),
+        means[3].astype(jnp.float32),
     )
 
 

time: 272 us -> 224 us (0.82)
  waiting for transfers between devices: 143 us -> 0 us
  Pallas kernels: 110 us -> 218 us
  between operations: 14 us -> 0.65 us
    psum x1 -> x0, waiting for transfers between devices: 143 us -> none  [body(): totals = lax.psum(tuple(states), 'row')]
    pallas_call x1, Pallas kernels: 110 us -> 218 us  [fused(): pl.pallas_call(functools.partial(fused_kernel, shards, replicas), out_sha...]
    mul x2 -> x0, other arithmetic: 5.21 us -> none  [body(): means = [total.astype(jnp.float32) * scale for total in totals]]
    convert_element_type x0 -> x2, other arithmetic: none -> 3.98 us  [the longest x1 2.63 us: body(): means[2].astype(jnp.float32)]
  transfers between devices with their start and end apart: 1 -> 0, of which waited for: 1 -> 0; matrix products, arithmetic and copies ran while one was open for 0% -> 0% of each run, Pallas kernels for 0% -> 0%
where the time goes in v2:
time: 224 us
  Pallas kernels  218 us (97%)
  other arithmetic  3.98 us (2%)
    pallas_call x1, Pallas kernels, fused(): pl.pallas_call(functools.partial(fused_kernel, shards, replicas), out_sha...  218 us

profile of v2, /device:TPU:0, one launch (start us, length us, event | category | flops | bytes accessed | tf_op | source)
XLA Modules:
  0.0 224.2 jit_solution(609005889123587478)
XLA Ops:
  0.6 217.5 %shard_map.93 = (bf16[2,896,256]{2,1,0:T(8,128)(2,1)}, bf16[2,256,896]{2,1,0:T(8,128)(2,1)}, bf16[2,896,256]{2,1,0:T(8,128)(2,1)}, bf16[2,256,896]{2,1,0:T(8,128)(2,1)}) custom-call(bf16[256,896]{1,0:T(8,128)(2,1)} %bitcast.10, bf16[256,896]{1,0:T(8,128)(2,1)} %bitcast.11, bf16[2,896,256]{2,1,0:T(8,128)(2,1)} %bitcast.8, bf16[2,256,896]{2,1,0:T(8,128)(2,1)} %bitcast.9, ...), custom_call_target="tpu_custom_call" | custom-call | tf_op jit(solution)/shard_map/pallas_call | solution.py:285
  218.2 0.0 copy-start.2
  218.2 2.6 %convert_element_type.6 = f32[2,896,256]{2,1,0:T(8,128)} convert(bf16[2,896,256]{2,1,0:T(8,128)(2,1)} %get-tuple-element.10) | non-fusion elementwise | flops 458752 | bytes 2752512 | tf_op jit(solution)/shard_map/convert_element_type | solution.py:354
  220.8 0.0 copy-done.2
  220.8 0.0 copy-start.1
  220.8 0.0 copy-start
  220.8 1.4 convert_element_type.7
  222.2 0.2 copy-done.1
  222.3 0.9 copy.12
  223.3 0.0 copy-done
  223.3 0.9 copy.13
Async XLA Ops:
  218.2 2.6 %copy-start.2 = (bf16[2,256,896]{2,1,0:T(8,128)(2,1)S(1)}, bf16[2,256,896]{2,1,0:T(8,128)(2,1)}, u32[]{:S(2)}) copy-start(bf16[2,256,896]{2,1,0:T(8,128)(2,1)} %get-tuple-element.11) | copy-start | bytes 2752516
  220.8 1.5 copy-start.1
  220.8 2.4 %copy-start = (bf16[2,256,896]{2,1,0:T(8,128)(2,1)S(1)}, bf16[2,256,896]{2,1,0:T(8,128)(2,1)}, u32[]{:S(2)}) copy-start(bf16[2,256,896]{2,1,0:T(8,128)(2,1)} %get-tuple-element.17) | copy-start | bytes 2752516

commit v3 on v2

--- a/solution.py
+++ b/solution.py
@@ -32,7 +32,7 @@
     shards, replicas,
     x0_ref, tg_ref, wd_in, wu_in, md_in, mu_in,
     wd_out, wu_out, md_out, mu_out,
-    wd, wu, md, mu, mdl, mul, res_wd, res_wu, res_md, res_mu,
+    wd, wu, md, mu, wdl, wul, mdl, mul, res_wd, res_wu, res_md, res_mu,
     got_wd, got_wu, got_md, got_mu, row_send, row_recv,
     x1, xt, gr, pre, act, inv, tot, sqs, low,
     s1, r1, s2, r2, s3, r3, q1, p1, q2, p2, q3, p3,
@@ -148,13 +148,15 @@
         lifted = dot_nn(activation, wu[layer]) * r_scale
         return (wide_rows + lifted).astype(jnp.bfloat16)
 
-    def update(w, m, layer, grad):
+    def update(w, m, layer, grad, last):
         moment = moment_decay * m[layer] + grad
         m[layer] = moment
+        if last and levels:
+            return
         w[layer] = (w[layer].astype(jnp.float32) - learn_rate * moment).astype(jnp.bfloat16)
 
-    def update_up(layer):
-        update(wu, mu, layer, dot_nn(act[layer].T, gr[...].astype(jnp.bfloat16)) * r_scale)
+    def update_up(layer, last):
+        update(wu, mu, layer, dot_nn(act[layer].T, gr[...].astype(jnp.bfloat16)) * r_scale, last)
 
     def low_grads(layer):
         preact = pre[layer]
@@ -163,18 +165,35 @@
         low[...] = (grad_pre * inv[layer]).astype(jnp.bfloat16)
         return jnp.sum(grad_pre * preact, axis=1, keepdims=True)
 
-    plain = list(bits)
-    swapped = plain[:2][::-1] + plain[2:]
-    down, up = (wd, got_wd, res_wd), (wu, got_wu, res_wu)
+    down, up = (wdl, got_wd, res_wd), (wul, got_wu, res_wu)
     mdown, mup = (mdl, got_md, res_md), (mul, got_mu, res_mu)
-    chunks = []
-    for layer in reversed(range(wd.shape[0])):
-        for group in ((up, mup), (down, mdown)):
-            for triple in group:
-                order = swapped if len(chunks) in (1, 4) else plain
-                chunks.append(triple + (layer, order))
-    late = [k for k, entry in enumerate(chunks) if entry[3] == 0 and (entry[0] is wd or entry[0] is mdl)]
-    early = [k for k in range(len(chunks)) if k not in late]
+    layers = list(reversed(range(wd.shape[0])))
+    chunks = [pair + (layer, bits) for layer in layers for pair in (up, down)]
+    first = len(chunks)
+    chunks += [pair + (layer, bits) for layer in layers for pair in (mup, mdown)]
+
+    def start(picked):
+        for chunk in picked if levels else []:
+            row_copy(chunk, 0).start()
+
+    def advance(slot):
+        for chunk in range(len(chunks)):
+            stage = slot - chunk
+            if not levels or stage < 0 or stage >= 2 * levels:
+                continue
+            row_copy(chunk, stage).wait_recv()
+            if stage < levels:
+                acc, got, res, layer, order = chunks[chunk]
+                size = acc.shape[1] >> (stage + 1)
+                keep = pl.ds(region(chunk, stage + 1), size)
+                landed = got.at[layer, pl.ds(acc.shape[1] - 2 * size, size)]
+                total = acc[layer, keep, :].astype(jnp.float32) + landed[...].astype(jnp.float32)
+                if stage < levels - 1:
+                    acc[layer, keep, :] = total.astype(jnp.bfloat16)
+                else:
+                    res[layer, keep, :] = (total * (1.0 / replicas)).astype(jnp.bfloat16)
+            if stage < 2 * levels - 1:
+                row_copy(chunk, stage + 1).start()
 
     def region(chunk, depth):
         acc, _, _, _, order = chunks[chunk]
@@ -204,37 +223,48 @@
             device_id={"row": row_peer[bit]}, device_id_type=MESH,
         )
 
-    def step(index, carry):
+    def step(last):
+        if last:
+            wdl[...] = wd[...]
+            wul[...] = wu[...]
+            start(range(first))
         x1[...] = forward(0, x0_ref[...], x0_ref[...].astype(jnp.float32))
         outcome = forward(1, x1[...], x1[...].astype(jnp.float32))
         gr[...] = outcome.astype(jnp.float32) - tg_ref[...].astype(jnp.float32)
 
+        def first_work():
+            update_up(1, last)
+            if last:
+                advance(0)
+
         partial_act = dot_nt(gr[...].astype(jnp.bfloat16), wu[1]) * r_scale
-        exchange(0, partial_act, None, lambda: update_up(1))
+        exchange(0, partial_act, None, first_work)
         row_dot = low_grads(1)
         through = dot_nt(low[...], wd[1]) * d_scale
         coefficient = row_dot * inv[1] * inv[1] / full
         gr[...] = gr[...] + through - coefficient * x1[...].astype(jnp.float32)
 
         def work():
-            update(wd, md, 1, dot_nn(x1[...].T, low[...]) * d_scale)
-            update_up(0)
-
-            @pl.when(index == STEPS - 1)
-            def _():
+            update(wd, md, 1, dot_nn(x1[...].T, low[...]) * d_scale, last)
+            update_up(0, last)
+            if last:
                 mul[...] = mu[...].astype(jnp.bfloat16)
                 mdl[1] = md[1].astype(jnp.bfloat16)
-                for chunk in early if levels else []:
-                    row_copy(chunk, 0).start()
+                start(range(first, len(chunks) - 1))
+                advance(1)
 
         partial_act = dot_nt(gr[...].astype(jnp.bfloat16), wu[0]) * r_scale
         exchange(1, partial_act, None, work)
         low_grads(0)
-        update(wd, md, 0, dot_nn(xt[...], low[...]) * d_scale)
+        update(wd, md, 0, dot_nn(xt[...], low[...]) * d_scale, last)
+
+    def middle(index, carry):
+        step(False)
         return carry
 
     xt[...] = x0_ref[...].T
-    lax.fori_loop(0, STEPS, step, 0)
+    lax.fori_loop(0, STEPS - 1, middle, 0)
+    step(True)
     mdl[0] = md[0].astype(jnp.bfloat16)
     if not levels:
         wd_out[...] = wd[...]
@@ -242,33 +272,19 @@
         md_out[...] = mdl[...]
         mu_out[...] = mul[...]
         return
-    for chunk in late:
-        row_copy(chunk, 0).start()
-
-    count = len(chunks)
-    for slot in range(count + 2 * levels - 1):
-        for chunk in range(count):
-            stage = slot - chunk
-            if stage < 0 or stage >= 2 * levels:
-                continue
-            row_copy(chunk, stage).wait_recv()
-            if stage < levels:
-                acc, got, res, layer, order = chunks[chunk]
-                size = acc.shape[1] >> (stage + 1)
-                keep = pl.ds(region(chunk, stage + 1), size)
-                landed = got.at[layer, pl.ds(acc.shape[1] - 2 * size, size)]
-                total = acc[layer, keep, :].astype(jnp.float32) + landed[...].astype(jnp.float32)
-                if stage < levels - 1:
-                    acc[layer, keep, :] = total.astype(jnp.bfloat16)
-                else:
-                    res[layer, keep, :] = (total * (1.0 / replicas)).astype(jnp.bfloat16)
-            if stage < 2 * levels - 1:
-                row_copy(chunk, stage + 1).start()
-    for chunk in range(count):
+    start([len(chunks) - 1])
+    for slot in range(2, len(chunks) + 2 * levels - 1):
+        advance(slot)
+    for chunk in range(len(chunks)):
         for stage in range(2 * levels):
             row_copy(chunk, stage).wait_send()
-    wd_out[...] = res_wd[...]
-    wu_out[...] = res_wu[...]
+
+    def stepped(weights, moments):
+        moved = weights.astype(jnp.float32) - learn_rate * moments.astype(jnp.float32)
+        return moved.astype(jnp.bfloat16)
+
+    wd_out[...] = stepped(res_wd[...], res_md[...])
+    wu_out[...] = stepped(res_wu[...], res_mu[...])
     md_out[...] = res_md[...]
     mu_out[...] = res_mu[...]
 
@@ -297,6 +313,8 @@
             pltpu.VMEM(w_up.shape, bf),
             pltpu.VMEM(m_down.shape, f32),
             pltpu.VMEM(m_up.shape, f32),
+            pltpu.VMEM(w_down.shape, bf),
+            pltpu.VMEM(w_up.shape, bf),
             pltpu.VMEM(m_down.shape, bf),
             pltpu.VMEM(m_up.shape, bf),
             pltpu.VMEM(w_down.shape, bf),

time: 224 us -> 188 us (0.84)
  Pallas kernels: 218 us -> 182 us
    pallas_call x1, Pallas kernels: 218 us -> 182 us  [fused(): pl.pallas_call(functools.partial(fused_kernel, shards, replicas), out_sha...]
where the time goes in v3:
time: 188 us
  Pallas kernels  182 us (97%)
  other arithmetic  3.98 us (2%)
  local copies, waits for them, and re-layouts  2.01 us (1%)
    pallas_call x1, Pallas kernels, fused(): pl.pallas_call(functools.partial(fused_kernel, shards, replicas), out_sha...  182 us

profile of v3, /device:TPU:0, one launch (start us, length us, event | category | flops | bytes accessed | tf_op | source)
XLA Modules:
  0.0 188.2 jit_solution(11492770754597337347)
XLA Ops:
  0.6 181.6 %shard_map.93 = (bf16[2,896,256]{2,1,0:T(8,128)(2,1)}, bf16[2,256,896]{2,1,0:T(8,128)(2,1)}, bf16[2,896,256]{2,1,0:T(8,128)(2,1)}, bf16[2,256,896]{2,1,0:T(8,128)(2,1)}) custom-call(bf16[256,896]{1,0:T(8,128)(2,1)} %bitcast.10, bf16[256,896]{1,0:T(8,128)(2,1)} %bitcast.11, bf16[2,896,256]{2,1,0:T(8,128)(2,1)} %bitcast.8, bf16[2,256,896]{2,1,0:T(8,128)(2,1)} %bitcast.9, ...), custom_call_target="tpu_custom_call" | custom-call | tf_op jit(solution)/shard_map/pallas_call | solution.py:301
  182.2 0.0 copy-start.2
  182.2 2.6 %convert_element_type.6 = f32[2,896,256]{2,1,0:T(8,128)} convert(bf16[2,896,256]{2,1,0:T(8,128)(2,1)} %get-tuple-element.10) | non-fusion elementwise | flops 458752 | bytes 2752512 | tf_op jit(solution)/shard_map/convert_element_type | solution.py:372
  184.9 0.0 copy-done.2
  184.9 0.0 copy-start.1
  184.9 0.0 copy-start
  184.9 1.4 convert_element_type.7
  186.2 0.2 copy-done.1
  186.4 0.9 copy.12
  187.3 0.0 copy-done
  187.3 0.9 copy.13
Async XLA Ops:
  182.2 2.6 %copy-start.2 = (bf16[2,256,896]{2,1,0:T(8,128)(2,1)S(1)}, bf16[2,256,896]{2,1,0:T(8,128)(2,1)}, u32[]{:S(2)}) copy-start(bf16[2,256,896]{2,1,0:T(8,128)(2,1)} %get-tuple-element.11) | copy-start | bytes 2752516
  184.9 1.5 copy-start.1
  184.9 2.4 %copy-start = (bf16[2,256,896]{2,1,0:T(8,128)(2,1)S(1)}, bf16[2,256,896]{2,1,0:T(8,128)(2,1)}, u32[]{:S(2)}) copy-start(bf16[2,256,896]{2,1,0:T(8,128)(2,1)} %get-tuple-element.17) | copy-start | bytes 2752516

commit v4 on v3

--- a/solution.py
+++ b/solution.py
@@ -136,9 +136,9 @@
         if squares is not None:
             sqs[other, :] = to_column(p3[...])
 
-    def forward(layer, rows, wide_rows):
+    def forward(layer, rows, wide_rows, work=None):
         squares = jnp.sum(wide_rows * wide_rows, axis=1, keepdims=True)
-        exchange(layer, dot_nn(rows, wd[layer]) * d_scale, squares, None)
+        exchange(layer, dot_nn(rows, wd[layer]) * d_scale, squares, work)
         inverse = lax.rsqrt(sqs[...] / full + norm_eps)
         preact = tot[...] * inverse
         activation = (preact * jax.nn.sigmoid(preact)).astype(jnp.bfloat16)
@@ -170,7 +170,12 @@
     layers = list(reversed(range(wd.shape[0])))
     chunks = [pair + (layer, bits) for layer in layers for pair in (up, down)]
     first = len(chunks)
-    chunks += [pair + (layer, bits) for layer in layers for pair in (mup, mdown)]
+    swapped = bits[:2][::-1] + bits[2:]
+    chunks += [
+        pair + (layer, swapped if layer == 0 and pair is mup else bits)
+        for layer in layers
+        for pair in (mup, mdown)
+    ]
 
     def start(picked):
         for chunk in picked if levels else []:
@@ -229,13 +234,15 @@
             wul[...] = wu[...]
             start(range(first))
         x1[...] = forward(0, x0_ref[...], x0_ref[...].astype(jnp.float32))
-        outcome = forward(1, x1[...], x1[...].astype(jnp.float32))
+        outcome = forward(
+            1, x1[...], x1[...].astype(jnp.float32), (lambda: advance(0)) if last else None
+        )
         gr[...] = outcome.astype(jnp.float32) - tg_ref[...].astype(jnp.float32)
 
         def first_work():
             update_up(1, last)
             if last:
-                advance(0)
+                advance(1)
 
         partial_act = dot_nt(gr[...].astype(jnp.bfloat16), wu[1]) * r_scale
         exchange(0, partial_act, None, first_work)
@@ -251,7 +258,7 @@
                 mul[...] = mu[...].astype(jnp.bfloat16)
                 mdl[1] = md[1].astype(jnp.bfloat16)
                 start(range(first, len(chunks) - 1))
-                advance(1)
+                advance(2)
 
         partial_act = dot_nt(gr[...].astype(jnp.bfloat16), wu[0]) * r_scale
         exchange(1, partial_act, None, work)
@@ -273,7 +280,7 @@
         mu_out[...] = mul[...]
         return
     start([len(chunks) - 1])
-    for slot in range(2, len(chunks) + 2 * levels - 1):
+    for slot in range(3, len(chunks) + 2 * levels - 1):
         advance(slot)
     for chunk in range(len(chunks)):
         for stage in range(2 * levels):

time: 188 us -> 186 us (0.989)
  Pallas kernels: 182 us -> 179 us
    pallas_call x1, Pallas kernels: 182 us -> 179 us  [fused(): pl.pallas_call(functools.partial(fused_kernel, shards, replicas), out_sha...]
where the time goes in v4:
time: 186 us
  Pallas kernels  179 us (96%)
  other arithmetic  3.98 us (2%)
  local copies, waits for them, and re-layouts  2.01 us (1%)
    pallas_call x1, Pallas kernels, fused(): pl.pallas_call(functools.partial(fused_kernel, shards, replicas), out_sha...  179 us

profile of v4, /device:TPU:0, one launch (start us, length us, event | category | flops | bytes accessed | tf_op | source)
XLA Modules:
  0.0 185.9 jit_solution(16541922913832497750)
XLA Ops:
  0.6 179.2 %shard_map.93 = (bf16[2,896,256]{2,1,0:T(8,128)(2,1)}, bf16[2,256,896]{2,1,0:T(8,128)(2,1)}, bf16[2,896,256]{2,1,0:T(8,128)(2,1)}, bf16[2,256,896]{2,1,0:T(8,128)(2,1)}) custom-call(bf16[256,896]{1,0:T(8,128)(2,1)} %bitcast.10, bf16[256,896]{1,0:T(8,128)(2,1)} %bitcast.11, bf16[2,896,256]{2,1,0:T(8,128)(2,1)} %bitcast.8, bf16[2,256,896]{2,1,0:T(8,128)(2,1)} %bitcast.9, ...), custom_call_target="tpu_custom_call" | custom-call | tf_op jit(solution)/shard_map/pallas_call | solution.py:308
  179.9 0.0 copy-start.2
  179.9 2.6 %convert_element_type.6 = f32[2,896,256]{2,1,0:T(8,128)} convert(bf16[2,896,256]{2,1,0:T(8,128)(2,1)} %get-tuple-element.10) | non-fusion elementwise | flops 458752 | bytes 2752512 | tf_op jit(solution)/shard_map/convert_element_type | solution.py:379
  182.5 0.0 copy-done.2
  182.5 0.0 copy-start.1
  182.5 0.0 copy-start
  182.5 1.4 convert_element_type.7
  183.9 0.2 copy-done.1
  184.0 0.9 copy.12
  184.9 0.0 copy-done
  184.9 0.9 copy.13
Async XLA Ops:
  179.9 2.6 %copy-start.2 = (bf16[2,256,896]{2,1,0:T(8,128)(2,1)S(1)}, bf16[2,256,896]{2,1,0:T(8,128)(2,1)}, u32[]{:S(2)}) copy-start(bf16[2,256,896]{2,1,0:T(8,128)(2,1)} %get-tuple-element.11) | copy-start | bytes 2752516
  182.5 1.5 copy-start.1
  182.5 2.4 %copy-start = (bf16[2,256,896]{2,1,0:T(8,128)(2,1)S(1)}, bf16[2,256,896]{2,1,0:T(8,128)(2,1)}, u32[]{:S(2)}) copy-start(bf16[2,256,896]{2,1,0:T(8,128)(2,1)} %get-tuple-element.17) | copy-start | bytes 2752516
